TPU v7x, 32 devices: a whole 2x2x4 slice. The times are simulated.
32 devices in a mesh: leaf: 2 (over core), row: 4 (over y, x), col: 4 (over z).
Axes of the slice: x: 2, y: 2, z: 4, core: 2. Of those that a mesh axis runs over, the one named last changes fastest.
Arguments:
- rhs_leaf: bfloat16 [2, 8, 64, 2048], P('leaf', None, None, 'col'), may hold values from -6 to 6
- dinv_leaf: bfloat16 [2, 8, 2048, 2048], P('leaf', None, 'row', 'col'), as said below
- panel_leaf: bfloat16 [2, 8, 1024, 2048], P('leaf', None, 'col', 'row'), may hold values from -0.0625 to 0.0625
- counts: int32 [2, 8], P('leaf'), may hold values from 256 to 2048, as said below
- row_index: int32 [2, 8, 1024], P('leaf'), may hold values from 0 to 4095, as said below
- rhs_root: bfloat16 [64, 4096], P(None, 'col'), may hold values from -6 to 6
- dinv_root: bfloat16 [4096, 4096], P(('leaf', 'row')), as said below
Outputs:
- y_leaf: bfloat16 [2, 8, 64, 2048], P('leaf', None, None, 'row')
- y_root: bfloat16 [64, 4096], P(None, ('leaf', 'row'))
Inputs may be any that keep to these rules, and one draw needn't show every extreme that they name: `counts`: each subtree supernode has at least 256 columns; at least one supernode of every draw has all 2048. `row_index`: within one supernode the 1024 entries are distinct and increasing. `dinv_leaf`: each [2048, 2048] block is lower triangular with a nonzero diagonal. `dinv_root`: lower triangular with a nonzero diagonal.
All inputs are finite; a program needn't handle non-finite values.
Results may differ from a plain program's by a relative error of at most 0.0053.
Values may be sent and summed in bfloat16 or wider, within the bound.
No kernel may reach another device: no remote copies, remote signals or barrier semaphores. Data moves between devices by JAX's collectives and lax.ppermute only.
A program may use at most 64 MiB of HBM per device.

v0:
```python
import jax
import jax.numpy as jnp
from jax import lax
from jax.sharding import PartitionSpec as P


def local(rhs_leaf, dinv_leaf, panel_leaf, counts, row_index, rhs_root, dinv_root):
    width_col = rhs_leaf.shape[3]
    width_row = dinv_leaf.shape[2]
    panel_rows = panel_leaf.shape[2]
    columns = rhs_root.shape[0]
    sep_width = rhs_root.shape[1] * lax.axis_size("col")
    limit = counts[0][:, None, None]
    col_slots = lax.axis_index("col") * width_col + lax.iota(jnp.int32, width_col)
    masked = jnp.where(col_slots[None, None, :] < limit, rhs_leaf[0], jnp.zeros((), jnp.bfloat16))
    partial_value = jnp.einsum(
        "kbj,kij->kbi", masked, dinv_leaf[0], preferred_element_type=jnp.float32
    )
    summed = lax.psum(partial_value, "col")
    row_slots = lax.axis_index("row") * width_row + lax.iota(jnp.int32, width_row)
    live_rows = (row_slots[None, None, :] < limit).astype(jnp.float32)
    solved = (summed * live_rows).astype(jnp.bfloat16)
    update = jnp.einsum("kbi,kri->kbr", solved, panel_leaf[0], preferred_element_type=jnp.float32)
    offset = lax.axis_index("col") * panel_rows
    targets = lax.dynamic_slice_in_dim(row_index[0], offset, panel_rows, 1)
    flat_update = jnp.transpose(update, (1, 0, 2)).reshape(columns, -1)
    accum = jnp.zeros((columns, sep_width), jnp.float32).at[:, targets.reshape(-1)].add(flat_update)
    piece = lax.psum_scatter(accum, "col", scatter_dimension=1, tiled=True)
    share = lax.psum(piece, ("leaf", "row"))
    reduced = (rhs_root.astype(jnp.float32) - share).astype(jnp.bfloat16)
    whole_reduced = lax.all_gather(reduced, "col", axis=1, tiled=True)
    y_root = jnp.dot(whole_reduced, dinv_root.T, preferred_element_type=jnp.float32).astype(
        jnp.bfloat16
    )
    return (solved[None], y_root)


def solution(mesh):
    in_specs = (
        P("leaf", None, None, "col"),
        P("leaf", None, "row", "col"),
        P("leaf", None, "col", "row"),
        P("leaf", None),
        P("leaf", None, None),
        P(None, "col"),
        P(("leaf", "row"), None),
    )
    out_specs = (P("leaf", None, None, "row"), P(None, ("leaf", "row")))
    return jax.shard_map(local, mesh=mesh, in_specs=in_specs, out_specs=out_specs, check_vma=False)
```

profile of v0, /device:TPU:0, one launch (start us, length us, event | category | flops | bytes accessed | tf_op | source)
XLA Modules:
  0.0 218.8 jit_solution(5079778243573968000)
XLA Ops:
  7.2 0.0 copy-start
  7.2 0.0 all-reduce.3.cloned.1.call-start
  7.2 0.9 compare_convert_fusion
  8.1 4.7 %fusion = f32[8,64,512]{2,1,0:T(8,128)} fusion(bf16[1,8,512,512]{3,2,1,0:T(8,128)(2,1)} %param.8, bf16[1,8,64,512]{3,2,1,0:T(8,128)(2,1)} %param.7, pred[8,512]{1,0:T(8,128)(4,1)S(1)} %get-tuple-element.3), kind=kOutput, calls=%fused_computation.1 | convolution fusion | flops 268697600 | bytes 5771264 | tf_op jit(solution)/shard_map/kbj,kij->kbi/dot_general | solution.py:16
  12.8 0.0 all-reduce.3.cloned.1.call-update
  12.8 0.0 reduce-scatter.2.cloned.1.call-start
  12.9 0.7 dynamic-slice_bitcast_fusion
  13.6 54.0 %all-reduce.3.cloned.1.call-done = f32[8,64,512]{2,1,0:T(8,128)} async-done(((f32[8,64,512]{2,1,0:T(8,128)}), f32[8,64,512]{2,1,0:T(8,128)}) %all-reduce.3.cloned.1.call-update) | async-done | bytes 1048592 | tf_op jit(solution)/shard_map/psum | solution.py:19
  67.6 0.0 copy-done
  67.6 2.0 fusion.4
  69.6 0.1 copy.13
  69.7 1.3 copy.12
  71.0 0.0 copy-start.2
  71.0 0.0 copy-start.1
  71.0 13.3 %scatter_custom_fusion = f32[64,4096]{0,1:T(8,128)} fusion(s32[2048]{0:T(1024)S(1)} %bitcast.29, f32[2048,64]{1,0:T(8,128)} %copy.12, f32[]{:T(128)} %constant.7.clone.1), kind=kCustom, calls=%fused_computation.7 | custom fusion | flops 131072 | bytes 1049088 | tf_op jit(solution)/shard_map/scatter-add | solution.py:27
  84.3 0.0 reduce-scatter.2.cloned.1.call-update
  84.3 0.0 all-reduce.5.cloned.1.call-start
  84.4 0.0 copy-done.2
  84.4 0.2 copy.10
  84.6 42.8 %reduce-scatter.2.cloned.1.call-done = f32[64,1024]{0,1:T(8,128)} async-done(((f32[64,4096]{0,1:T(8,128)}), f32[64,1024]{0,1:T(8,128)}) %reduce-scatter.2.cloned.1.call-update) | async-done | bytes 262160 | tf_op jit(solution)/shard_map/reduce_scatter | solution.py:28
  127.4 0.0 all-reduce.5.cloned.1.call-update
  127.4 0.0 copy-done.1
  127.4 0.9 fusion.11
  128.4 56.2 %all-reduce.5.cloned.1.call-done = f32[64,1024]{0,1:T(8,128)} async-done(((f32[64,1024]{0,1:T(8,128)}), f32[64,1024]{0,1:T(8,128)}) %all-reduce.5.cloned.1.call-update) | async-done | bytes 262160 | tf_op jit(solution)/shard_map/psum | solution.py:29
  184.5 1.1 subtract_convert_fusion
  185.6 22.4 %all_gather.3 = bf16[64,4096]{0,1:T(8,128)(2,1)S(1)} all-gather(bf16[64,1024]{0,1:T(8,128)(2,1)S(1)} %subtract_convert_fusion), channel_id=1, replica_groups=mesh['leaf'=2,'row'=4,'col'=4] {'col'}, dimensions={1}, use_global_device_ids=true | all-gather | bytes 655360 | tf_op jit(solution)/shard_map/all_gather | solution.py:31
  208.0 4.2 %convolution_convert_fusion = bf16[64,512]{1,0:T(8,128)(2,1)} fusion(bf16[64,4096]{0,1:T(8,128)(2,1)S(1)} %all_gather.3, bf16[512,4096]{1,0:T(8,128)(2,1)} %param.13), kind=kOutput, calls=%fused_computation.6 | convolution fusion | flops 268468224 | bytes 4784128 | tf_op jit(solution)/shard_map/dot_general | solution.py:32
  (3 shorter events, 0.0 us)
Async XLA Ops:
  7.2 60.5 %copy-start = (bf16[1,8,256,512]{3,2,1,0:T(8,128)(2,1)S(1)}, bf16[1,8,256,512]{3,2,1,0:T(8,128)(2,1)}, u32[]{:S(2)}) copy-start(bf16[1,8,256,512]{3,2,1,0:T(8,128)(2,1)} %param.9) | copy-start | bytes 6291460
  7.2 60.4 %all-reduce.3.cloned.1.call-start = ((), (), s32[]{:S(2)}) async-start(), calls=%async_computation.1 | async-start | bytes 2097152 | tf_op jit(solution)/shard_map/psum | solution.py:19
  12.8 114.6 %reduce-scatter.2.cloned.1.call-start = ((), (), s32[]{:S(2)}) async-start(), calls=%async_computation.2 | async-start | bytes 2621440 | tf_op jit(solution)/shard_map/reduce_scatter | solution.py:28
  71.0 13.4 %copy-start.2 = (bf16[64,1024]{1,0:T(8,128)(2,1)S(1)}, bf16[64,1024]{1,0:T(8,128)(2,1)}, u32[]{:S(2)}) copy-start(bf16[64,1024]{1,0:T(8,128)(2,1)} %param.12) | copy-start | bytes 393220
  71.0 56.5 %copy-start.1 = (f32[8,64,512]{2,1,0:T(8,128)S(1)}, f32[8,64,512]{2,1,0:T(8,128)}, u32[]{:S(2)}) copy-start(f32[8,64,512]{2,1,0:T(8,128)} %all-reduce.3.cloned.1.call-done) | copy-start | bytes 3145732
  84.3 100.2 %all-reduce.5.cloned.1.call-start = ((), (), s32[]{:S(2)}) async-start(), calls=%async_computation.3 | async-start | bytes 1048576 | tf_op jit(solution)/shard_map/psum | solution.py:29
Sparse Core Ops, SparseCore 0:
  13.0 54.6 all-reduce.2
  84.5 42.8 reduce-scatter.1
  130.5 53.9 all-reduce.4
where the time goes:
time: 219 us
  waiting for transfers between devices  153 us (70%)
  blocking collectives  22.4 us (10%)
  other arithmetic  16.2 us (7%)
  between operations  13.8 us (6%)
  matrix products  10.9 us (5%)
  local copies, waits for them, and re-layouts  2.27 us (1%)
    psum x1, waiting for transfers between devices, local(): share = lax.psum(piece, ('leaf', 'row'))  56.2 us
    psum x1, waiting for transfers between devices, local(): summed = lax.psum(partial_value, 'col')  54 us
    reduce_scatter x1, waiting for transfers between devices, local(): piece = lax.psum_scatter(accum, 'col', scatter_dimension=1, tiled=True)  42.8 us
    all_gather x1, blocking collectives, local(): whole_reduced = lax.all_gather(reduced, 'col', axis=1, tiled=True)  22.4 us
    scatter-add x1, other arithmetic, local(): jnp.zeros((columns, sep_width), jnp.float32).at[:, targets.reshape(-1)]  13.3 us
    dot_general x1, matrix products, local(): jnp.einsum('kbj,kij->kbi', masked, dinv_leaf[0], preferred_element_type=j...  4.71 us
  transfers between devices with their start and end apart: 3, of which 3 were waited for; matrix products, arithmetic and copies ran while one was open for 1% of the time, Pallas kernels for 0%

commit v1 on v0

--- a/solution.py
+++ b/solution.py
@@ -1,7 +1,19 @@
+import functools
 import jax
 import jax.numpy as jnp
 from jax import lax
 from jax.sharding import PartitionSpec as P
+
+
+def area_spread(block_here, axis_key, dim_no):
+    parts_out = lax.axis_size(axis_key)
+    t_next = jnp.stack(parts_out * [block_here], axis=0)
+    f_now = lax.all_to_all(t_next, axis_name=axis_key, split_axis=0, concat_axis=0)
+    plain = jnp.concatenate(f_now, dim_no)
+    return plain
+
+
+put_counts = functools.partial(area_spread, axis_key="col", dim_no=1)
 
 
 def local(rhs_leaf, dinv_leaf, panel_leaf, counts, row_index, rhs_root, dinv_root):
@@ -28,7 +40,7 @@
     piece = lax.psum_scatter(accum, "col", scatter_dimension=1, tiled=True)
     share = lax.psum(piece, ("leaf", "row"))
     reduced = (rhs_root.astype(jnp.float32) - share).astype(jnp.bfloat16)
-    whole_reduced = lax.all_gather(reduced, "col", axis=1, tiled=True)
+    whole_reduced = put_counts(reduced)
     y_root = jnp.dot(whole_reduced, dinv_root.T, preferred_element_type=jnp.float32).astype(
         jnp.bfloat16
     )

time: 219 us -> 202 us (0.922)
  blocking collectives: 22.4 us -> 0 us
  local copies, waits for them, and re-layouts: 2.27 us -> 7.24 us
  starting transfers between devices: 0.12 us -> 4.72 us
  waiting for transfers between devices: 153 us -> 149 us
    all_gather x1 -> x0, blocking collectives: 22.4 us -> none  [local(): whole_reduced = lax.all_gather(reduced, 'col', axis=1, tiled=True)]
    reduce_scatter x1, waiting for transfers between devices: 42.8 us -> 26.7 us  [local(): piece = lax.psum_scatter(accum, 'col', scatter_dimension=1, tiled=True)]
    all_to_all x0 -> x1, waiting for transfers between devices: none -> 12.9 us  [area_spread(): lax.all_to_all(t_next, axis_name=axis_key, split_axis=0, concat_axis=0)]
    all_to_all x0 -> x1, starting transfers between devices: none -> 4.6 us  [area_spread(): lax.all_to_all(t_next, axis_name=axis_key, split_axis=0, concat_axis=0)]
    scatter-add x0 -> x1, local copies, waits for them, and re-layouts: none -> 3.2 us  [local(): jnp.zeros((columns, sep_width), jnp.float32).at[:, targets.reshape(-1)]]
  transfers between devices with their start and end apart: 3 -> 4, of which waited for: 3 -> 4; matrix products, arithmetic and copies ran while one was open for 1% -> 1% of each run, Pallas kernels for 0% -> 0%
where the time goes in v1:
time: 202 us
  waiting for transfers between devices  149 us (74%)
  other arithmetic  16 us (8%)
  between operations  13.8 us (7%)
  matrix products  10.9 us (5%)
  local copies, waits for them, and re-layouts  7.24 us (4%)
  starting transfers between devices  4.72 us (2%)
    psum x1, waiting for transfers between devices, local(): share = lax.psum(piece, ('leaf', 'row'))  55.4 us
    psum x1, waiting for transfers between devices, local(): summed = lax.psum(partial_value, 'col')  54 us
    reduce_scatter x1, waiting for transfers between devices, local(): piece = lax.psum_scatter(accum, 'col', scatter_dimension=1, tiled=True)  26.7 us
    scatter-add x1, other arithmetic, local(): jnp.zeros((columns, sep_width), jnp.float32).at[:, targets.reshape(-1)]  13.2 us
    all_to_all x1, waiting for transfers between devices, area_spread(): lax.all_to_all(t_next, axis_name=axis_key, split_axis=0, concat_axis=0)  12.9 us
    dot_general x1, matrix products, local(): jnp.einsum('kbj,kij->kbi', masked, dinv_leaf[0], preferred_element_type=j...  4.7 us
    all_to_all x1, starting transfers between devices, area_spread(): lax.all_to_all(t_next, axis_name=axis_key, split_axis=0, concat_axis=0)  4.6 us
    dot_general x1, matrix products, local(): jnp.dot(whole_reduced, dinv_root.T, preferred_element_type=jnp.float32)  4.23 us
  transfers between devices with their start and end apart: 4, of which 4 were waited for; matrix products, arithmetic and copies ran while one was open for 1% of the time, Pallas kernels for 0%

profile of v1, /device:TPU:0, one launch (start us, length us, event | category | flops | bytes accessed | tf_op | source)
XLA Modules:
  0.0 201.7 jit_solution(159280099886812826)
XLA Ops:
  7.2 0.0 copy-start
  7.2 0.0 all-reduce.3.cloned.1.call-start
  7.2 0.9 compare_convert_fusion
  8.1 4.7 %fusion = f32[8,64,512]{2,1,0:T(8,128)} fusion(bf16[1,8,512,512]{3,2,1,0:T(8,128)(2,1)} %param.8, bf16[1,8,64,512]{3,2,1,0:T(8,128)(2,1)} %param.7, pred[8,512]{1,0:T(8,128)(4,1)S(1)} %get-tuple-element.3), kind=kOutput, calls=%fused_computation.1 | convolution fusion | flops 268697600 | bytes 5771264 | tf_op jit(solution)/shard_map/kbj,kij->kbi/dot_general | solution.py:28
  12.8 0.0 all-reduce.3.cloned.1.call-update
  12.8 0.0 reduce-scatter.2.cloned.1.call-start
  12.9 0.7 dynamic-slice_bitcast_fusion
  13.6 54.0 %all-reduce.3.cloned.1.call-done = f32[8,64,512]{2,1,0:T(8,128)} async-done(((f32[8,64,512]{2,1,0:T(8,128)}), f32[8,64,512]{2,1,0:T(8,128)}) %all-reduce.3.cloned.1.call-update) | async-done | bytes 1048592 | tf_op jit(solution)/shard_map/psum | solution.py:31
  67.6 0.0 copy-done
  67.6 2.0 fusion.4
  69.6 0.1 copy.24
  69.7 1.3 copy.21
  71.0 13.2 %scatter_custom_fusion = f32[64,4096]{0,1:T(8,128)} fusion(s32[2048]{0:T(1024)S(1)} %bitcast.33, f32[2048,64]{1,0:T(8,128)} %copy.21, f32[]{:T(128)} %constant.7.clone.1), kind=kCustom, calls=%fused_computation.7 | custom fusion | flops 131072 | bytes 1049088 | tf_op jit(solution)/shard_map/scatter-add | solution.py:39
  84.2 0.0 copy-start.2
  84.2 3.2 %copy.22 = f32[64,4096]{1,0:T(8,128)} copy(f32[64,4096]{0,1:T(8,128)} %scatter_custom_fusion) | data formatting | bytes 2097152 | tf_op jit(solution)/shard_map/scatter-add | solution.py:39
  87.4 0.0 copy-start.1
  87.4 0.0 reduce-scatter.2.cloned.1.call-update
  87.4 0.0 all-reduce.5.cloned.1.call-start
  87.5 26.7 %reduce-scatter.2.cloned.1.call-done = f32[64,1024]{1,0:T(8,128)} async-done(((f32[64,4096]{1,0:T(8,128)}), f32[64,1024]{1,0:T(8,128)}) %reduce-scatter.2.cloned.1.call-update) | async-done | bytes 262160 | tf_op jit(solution)/shard_map/reduce_scatter | solution.py:40
  114.2 0.0 all-reduce.5.cloned.1.call-update
  114.2 55.4 %all-reduce.5.cloned.1.call-done = f32[64,1024]{1,0:T(8,128)} async-done(((f32[64,1024]{1,0:T(8,128)}), f32[64,1024]{1,0:T(8,128)}) %all-reduce.5.cloned.1.call-update) | async-done | bytes 262160 | tf_op jit(solution)/shard_map/psum | solution.py:41
  169.6 0.0 copy-done.2
  169.6 1.0 subtract_convert_fusion
  170.6 0.9 stack.2
  171.5 4.6 %all-to-all-start = ((bf16[4,64,1024]{2,1,0:T(8,128)(2,1)}), bf16[4,64,1024]{2,1,0:T(8,128)(2,1)}, u32[]{:S(2)}, u32[]{:S(2)}) async-start(bf16[4,64,1024]{2,1,0:T(8,128)(2,1)} %stack.2), calls=%async_computation.1 | async-start | bytes 1048576 | tf_op jit(solution)/shard_map/all_to_all | solution.py:11
  176.1 0.0 copy-done.1
  176.1 0.9 fusion.11
  177.0 12.9 %all-to-all-done = bf16[4,64,1024]{2,1,0:T(8,128)(2,1)} async-done(((bf16[4,64,1024]{2,1,0:T(8,128)(2,1)}), bf16[4,64,1024]{2,1,0:T(8,128)(2,1)}, u32[]{:S(2)}, u32[]{:S(2)}) %all-to-all-start) | async-done | bytes 524320 | tf_op jit(solution)/shard_map/all_to_all | solution.py:11
  189.8 1.1 copy.25
  190.9 4.2 %convolution_convert_fusion = bf16[64,512]{1,0:T(8,128)(2,1)} fusion(bf16[64,4096]{1,0:T(8,128)(2,1)S(1)} %bitcast.31, bf16[512,4096]{1,0:T(8,128)(2,1)} %param.13), kind=kOutput, calls=%fused_computation.6 | convolution fusion | flops 268468224 | bytes 4784128 | tf_op jit(solution)/shard_map/dot_general | solution.py:44
  (3 shorter events, 0.0 us)
Async XLA Ops:
  7.2 60.5 %copy-start = (bf16[1,8,256,512]{3,2,1,0:T(8,128)(2,1)S(1)}, bf16[1,8,256,512]{3,2,1,0:T(8,128)(2,1)}, u32[]{:S(2)}) copy-start(bf16[1,8,256,512]{3,2,1,0:T(8,128)(2,1)} %param.9) | copy-start | bytes 6291460
  7.2 60.4 %all-reduce.3.cloned.1.call-start = ((), (), s32[]{:S(2)}) async-start(), calls=%async_computation.2 | async-start | bytes 2097152 | tf_op jit(solution)/shard_map/psum | solution.py:31
  12.8 101.3 %reduce-scatter.2.cloned.1.call-start = ((), (), s32[]{:S(2)}) async-start(), calls=%async_computation.3 | async-start | bytes 1310720 | tf_op jit(solution)/shard_map/reduce_scatter | solution.py:40
  84.2 85.4 %copy-start.2 = (bf16[64,1024]{1,0:T(8,128)(2,1)S(1)}, bf16[64,1024]{1,0:T(8,128)(2,1)}, u32[]{:S(2)}) copy-start(bf16[64,1024]{1,0:T(8,128)(2,1)} %param.12) | copy-start | bytes 393220
  87.4 88.6 %copy-start.1 = (f32[8,64,512]{2,1,0:T(8,128)S(1)}, f32[8,64,512]{2,1,0:T(8,128)}, u32[]{:S(2)}) copy-start(f32[8,64,512]{2,1,0:T(8,128)} %all-reduce.3.cloned.1.call-done) | copy-start | bytes 3145732
  87.4 82.2 %all-reduce.5.cloned.1.call-start = ((), (), s32[]{:S(2)}) async-start(), calls=%async_computation.4 | async-start | bytes 524288 | tf_op jit(solution)/shard_map/psum | solution.py:41
  171.5 18.4 %all-to-all-start = ((bf16[4,64,1024]{2,1,0:T(8,128)(2,1)}), bf16[4,64,1024]{2,1,0:T(8,128)(2,1)}, u32[]{:S(2)}, u32[]{:S(2)}) async-start(bf16[4,64,1024]{2,1,0:T(8,128)(2,1)} %stack.2), calls=%async_computation.1 | async-start | bytes 1048576 | tf_op jit(solution)/shard_map/all_to_all | solution.py:11
Sparse Core Ops, SparseCore 0:
  13.0 54.6 all-reduce.2
  87.6 26.5 reduce-scatter.1
  117.2 52.3 all-reduce.4
